TPU v7x, 32 devices: a whole 2x2x4 slice. The times are simulated.
32 devices in a mesh: dp: 8 (over y, x, core), mp: 4 (over z).
Axes of the slice: x: 2, y: 2, z: 4, core: 2. Of those that a mesh axis runs over, the one named last changes fastest.
Arguments:
- hidden: bfloat16 [8192, 2048], P('dp'), may hold values from -6 to 6
- cotangent: bfloat16 [8192, 2048], P('dp'), may hold values from -6 to 6
- lengths: int32 [16], P('dp'), may hold values from 64 to 512, as said below
- input_gain: bfloat16 [2048], P('dp'), may hold values from 0.5 to 1.5
- input_shift: bfloat16 [2048], P('dp'), may hold values from -1.25 to 1.25
- triple_weight: bfloat16 [2048, 3, 2048], P('dp', None, 'mp'), may hold values from -0.125 to 0.125
- triple_bias: bfloat16 [2, 2048], P(None, 'mp'), may hold values from -1.25 to 1.25
- merge_weight: bfloat16 [2048, 2048], P('mp', 'dp'), may hold values from -0.5 to 0.5
- merge_bias: bfloat16 [2048], P('dp'), may hold values from -1.25 to 1.25
- middle_gain: bfloat16 [2048], P('dp'), may hold values from 0.5 to 1.5
- middle_shift: bfloat16 [2048], P('dp'), may hold values from -1.25 to 1.25
- expand_weight: bfloat16 [2048, 8192], P('dp', 'mp'), may hold values from -0.125 to 0.125
- expand_bias: bfloat16 [8192], P('mp'), may hold values from -1.25 to 1.25
- reduce_weight: bfloat16 [8192, 2048], P('mp', 'dp'), may hold values from -0.0625 to 0.0625
- reduce_bias: bfloat16 [2048], P('dp'), may hold values from -1.25 to 1.25
Outputs:
- layer_output: bfloat16 [8192, 2048], P('dp')
- hidden_grad: bfloat16 [8192, 2048], P('dp')
- input_gain_grad: float32 [2048], P('dp')
- input_shift_grad: float32 [2048], P('dp')
- triple_weight_grad: float32 [2048, 3, 2048], P('dp', None, 'mp')
- triple_bias_grad: float32 [2, 2048], P(None, 'mp')
- merge_weight_grad: float32 [2048, 2048], P('mp', 'dp')
- merge_bias_grad: float32 [2048], P('dp')
- middle_gain_grad: float32 [2048], P('dp')
- middle_shift_grad: float32 [2048], P('dp')
- expand_weight_grad: float32 [2048, 8192], P('dp', 'mp')
- expand_bias_grad: float32 [8192], P('mp')
- reduce_weight_grad: float32 [8192, 2048], P('mp', 'dp')
- reduce_bias_grad: float32 [2048], P('dp')
- branch_rms: float32 [3], replicated
Inputs may be any that keep to these rules, and one draw needn't show every extreme that they name: `lengths`: each slot's valid tokens stand at its start; in every draw some slot is full (512 valid tokens).
All inputs are finite; a program needn't handle non-finite values.
Results may differ from a plain program's by a relative error of at most 0.023.
Values may be sent and summed in bfloat16 or wider, within the bound.
A program may use at most 256 MiB of HBM per device.

v0:
```python
import jax
import jax.numpy as jnp
from jax import lax
from jax.sharding import PartitionSpec as P

HEADS = 32
HEAD_DIM = 64
SLOT = 512
MICRO = 2


def layer_norm(values, gain_vec, shift_vec):
    center = values - jnp.mean(values, axis=-1, keepdims=True)
    spread = jnp.mean(center * center, axis=-1, keepdims=True)
    return center * lax.rsqrt(spread + 1e-05) * gain_vec + shift_vec


def gelu_exact(values):
    return jax.nn.gelu(values, approximate=False)


def attention_scores(query_low, key_low, slopes, length):
    raw_scores = jnp.einsum("qhe,khe->hqk", query_low, key_low, preferred_element_type=jnp.float32)
    places = jnp.arange(query_low.shape[0], dtype=jnp.int32)
    key_place = places.astype(jnp.float32)
    scores = (raw_scores + slopes[:, None, None] * key_place[None, None, :]) * 0.125
    allowed = (places[None, :] <= places[:, None]) & (places[None, :] < length)
    return jnp.where(allowed[None], scores, -1000000000.0)


def local(
    hidden,
    cotangent,
    lengths,
    input_gain,
    input_shift,
    triple_weight,
    triple_bias,
    merge_weight,
    merge_bias,
    middle_gain,
    middle_shift,
    expand_weight,
    expand_bias,
    reduce_weight,
    reduce_bias,
):
    slot = SLOT
    width = hidden.shape[1]
    head_cols = triple_weight.shape[2]
    unit_cols = expand_weight.shape[1]
    local_heads = head_cols // HEAD_DIM
    head_start = lax.axis_index("mp") * local_heads
    slopes = 2.0 ** (
        -8.0
        * (head_start + jnp.arange(local_heads, dtype=jnp.int32) + 1).astype(jnp.float32)
        / HEADS
    )
    bias_pair = triple_bias.astype(jnp.float32)
    unit_shift = expand_bias.astype(jnp.float32)
    attention_kept = (
        lax.all_gather(input_gain, "dp", axis=0, tiled=True),
        lax.all_gather(input_shift, "dp", axis=0, tiled=True),
        lax.all_gather(triple_weight, "dp", axis=0, tiled=True),
        lax.all_gather(merge_weight, "dp", axis=1, tiled=True),
        lax.all_gather(merge_bias, "dp", axis=0, tiled=True),
    )
    feed_kept = (
        lax.all_gather(middle_gain, "dp", axis=0, tiled=True),
        lax.all_gather(middle_shift, "dp", axis=0, tiled=True),
        lax.all_gather(expand_weight, "dp", axis=0, tiled=True),
        lax.all_gather(reduce_weight, "dp", axis=1, tiled=True),
        lax.all_gather(reduce_bias, "dp", axis=0, tiled=True),
    )
    acc_triple = jnp.zeros((width, 3, head_cols), jnp.float32)
    acc_merge = jnp.zeros((head_cols, width), jnp.float32)
    acc_expand = jnp.zeros((width, unit_cols), jnp.float32)
    acc_reduce = jnp.zeros((unit_cols, width), jnp.float32)
    acc_gain_one = jnp.zeros((width,), jnp.float32)
    acc_shift_one = jnp.zeros((width,), jnp.float32)
    acc_merge_bias = jnp.zeros((width,), jnp.float32)
    acc_gain_two = jnp.zeros((width,), jnp.float32)
    acc_shift_two = jnp.zeros((width,), jnp.float32)
    acc_reduce_bias = jnp.zeros((width,), jnp.float32)
    acc_pair_bias = jnp.zeros((2, head_cols), jnp.float32)
    acc_unit_bias = jnp.zeros((unit_cols,), jnp.float32)
    square_sums = jnp.zeros((4,), jnp.float32)
    output_parts = []
    grad_parts = []
    for batch_index in range(MICRO):
        start = batch_index * slot
        token_rows = hidden[start : start + slot].astype(jnp.float32)
        length = lengths[batch_index]
        valid_rows = (jnp.arange(slot, dtype=jnp.int32) < length)[:, None]
        gain_one, shift_one, triple_full, merge_full, merge_shift = attention_kept
        gain_two, shift_two, expand_full, reduce_full, reduce_shift = feed_kept
        gain_one = gain_one.astype(jnp.float32)
        shift_one = shift_one.astype(jnp.float32)
        gain_two = gain_two.astype(jnp.float32)
        shift_two = shift_two.astype(jnp.float32)
        norm_in = layer_norm(token_rows, gain_one, shift_one).astype(jnp.bfloat16)
        triple = jnp.einsum("td,dcf->tcf", norm_in, triple_full, preferred_element_type=jnp.float32)
        query_low = (
            (triple[:, 0] + bias_pair[0]).astype(jnp.bfloat16).reshape(slot, local_heads, HEAD_DIM)
        )
        key_low = triple[:, 1].astype(jnp.bfloat16).reshape(slot, local_heads, HEAD_DIM)
        value_low = (
            (triple[:, 2] + bias_pair[1]).astype(jnp.bfloat16).reshape(slot, local_heads, HEAD_DIM)
        )
        scores = attention_scores(query_low, key_low, slopes, length)
        log_total = jax.nn.logsumexp(scores, axis=-1)
        attention_weights = jnp.exp(scores - log_total[..., None]).astype(jnp.bfloat16)
        mixed_heads = jnp.einsum(
            "hqk,khe->qhe", attention_weights, value_low, preferred_element_type=jnp.float32
        )
        mixed_heads = mixed_heads.reshape(slot, head_cols).astype(jnp.bfloat16)
        attention_part = jnp.dot(mixed_heads, merge_full, preferred_element_type=jnp.float32)
        attention_branch = lax.psum(attention_part.astype(jnp.bfloat16), "mp").astype(
            jnp.float32
        ) + merge_shift.astype(jnp.float32)
        residual = token_rows + attention_branch
        norm_mid = layer_norm(residual, gain_two, shift_two).astype(jnp.bfloat16)
        token_count = length.astype(jnp.float32)
        expand_pre = jnp.dot(norm_mid, expand_full, preferred_element_type=jnp.float32) + unit_shift
        activation = gelu_exact(expand_pre).astype(jnp.bfloat16)
        feed_part = jnp.dot(activation, reduce_full, preferred_element_type=jnp.float32)
        feed_branch = lax.psum(feed_part.astype(jnp.bfloat16), "mp").astype(
            jnp.float32
        ) + reduce_shift.astype(jnp.float32)
        result = residual + feed_branch
        output_parts.append(jnp.where(valid_rows, result, 0.0).astype(jnp.bfloat16))
        square_sums = square_sums + jnp.stack(
            [
                jnp.sum(jnp.where(valid_rows, result * result, 0.0)),
                jnp.sum(jnp.where(valid_rows, attention_branch * attention_branch, 0.0)),
                jnp.sum(jnp.where(valid_rows, feed_branch * feed_branch, 0.0)),
                token_count,
            ]
        )
        grad_out = jnp.where(valid_rows, cotangent[start : start + slot].astype(jnp.float32), 0.0)
        grad_feed = grad_out.astype(jnp.bfloat16)
        acc_reduce_bias = acc_reduce_bias + jnp.sum(grad_out, axis=0)
        acc_reduce = acc_reduce + jnp.dot(
            activation.T, grad_feed, preferred_element_type=jnp.float32
        )
        grad_act = jnp.dot(grad_feed, reduce_full.T, preferred_element_type=jnp.float32)
        gelu_value, gelu_back = jax.vjp(gelu_exact, expand_pre)
        grad_pre = gelu_back(grad_act)[0].astype(jnp.bfloat16)
        acc_unit_bias = acc_unit_bias + jnp.sum(grad_pre, axis=0, dtype=jnp.float32)
        acc_expand = acc_expand + jnp.dot(norm_mid.T, grad_pre, preferred_element_type=jnp.float32)
        mid_part = jnp.dot(grad_pre, expand_full.T, preferred_element_type=jnp.float32)
        grad_mid = lax.psum(mid_part.astype(jnp.bfloat16), "mp").astype(jnp.float32)
        norm_value, norm_back = jax.vjp(layer_norm, residual, gain_two, shift_two)
        grad_resid_norm, grad_gain_two, grad_shift_two = norm_back(grad_mid)
        acc_gain_two = acc_gain_two + grad_gain_two
        acc_shift_two = acc_shift_two + grad_shift_two
        grad_residual = grad_out + grad_resid_norm
        grad_branch = grad_residual.astype(jnp.bfloat16)
        acc_merge_bias = acc_merge_bias + jnp.sum(grad_branch, axis=0, dtype=jnp.float32)
        acc_merge = acc_merge + jnp.dot(
            mixed_heads.T, grad_branch, preferred_element_type=jnp.float32
        )
        grad_mixed = jnp.dot(grad_branch, merge_full.T, preferred_element_type=jnp.float32)
        grad_mixed = grad_mixed.astype(jnp.bfloat16).reshape(slot, local_heads, HEAD_DIM)
        again_scores = attention_scores(query_low, key_low, slopes, length)
        soft_weights = jnp.exp(again_scores - log_total[..., None])
        grad_probs = jnp.einsum(
            "qhe,khe->hqk", grad_mixed, value_low, preferred_element_type=jnp.float32
        )
        grad_value = jnp.einsum(
            "hqk,qhe->khe",
            soft_weights.astype(jnp.bfloat16),
            grad_mixed,
            preferred_element_type=jnp.float32,
        ).astype(jnp.bfloat16)
        row_terms = jnp.sum(soft_weights * grad_probs, axis=-1, keepdims=True)
        grad_scores = (soft_weights * (grad_probs - row_terms)).astype(jnp.bfloat16)
        grad_query = (
            0.125
            * jnp.einsum("hqk,khe->qhe", grad_scores, key_low, preferred_element_type=jnp.float32)
        ).astype(jnp.bfloat16)
        grad_key = (
            0.125
            * jnp.einsum("hqk,qhe->khe", grad_scores, query_low, preferred_element_type=jnp.float32)
        ).astype(jnp.bfloat16)
        grad_triple = jnp.stack([grad_query, grad_key, grad_value], axis=1).reshape(
            slot, 3, head_cols
        )
        acc_pair_bias = acc_pair_bias + jnp.stack(
            [
                jnp.sum(grad_triple[:, 0], axis=0, dtype=jnp.float32),
                jnp.sum(grad_triple[:, 2], axis=0, dtype=jnp.float32),
            ]
        )
        acc_triple = acc_triple + jnp.einsum(
            "td,tcf->dcf", norm_in, grad_triple, preferred_element_type=jnp.float32
        )
        grad_in_part = jnp.einsum(
            "tcf,dcf->td", grad_triple, triple_full, preferred_element_type=jnp.float32
        )
        grad_in = lax.psum(grad_in_part.astype(jnp.bfloat16), "mp").astype(jnp.float32)
        first_value, first_back = jax.vjp(layer_norm, token_rows, gain_one, shift_one)
        grad_rows_norm, grad_gain_one, grad_shift_one = first_back(grad_in)
        acc_gain_one = acc_gain_one + grad_gain_one
        acc_shift_one = acc_shift_one + grad_shift_one
        input_rows_grad = (grad_residual + grad_rows_norm).astype(jnp.bfloat16)
        grad_parts.append(input_rows_grad)
    owned = (
        lax.psum_scatter(
            acc_triple.astype(jnp.bfloat16), "dp", scatter_dimension=0, tiled=True
        ).astype(jnp.float32),
        lax.psum_scatter(
            acc_merge.astype(jnp.bfloat16), "dp", scatter_dimension=1, tiled=True
        ).astype(jnp.float32),
        lax.psum_scatter(
            acc_expand.astype(jnp.bfloat16), "dp", scatter_dimension=0, tiled=True
        ).astype(jnp.float32),
        lax.psum_scatter(
            acc_reduce.astype(jnp.bfloat16), "dp", scatter_dimension=1, tiled=True
        ).astype(jnp.float32),
        lax.psum_scatter(
            acc_gain_one.astype(jnp.bfloat16), "dp", scatter_dimension=0, tiled=True
        ).astype(jnp.float32),
        lax.psum_scatter(
            acc_shift_one.astype(jnp.bfloat16), "dp", scatter_dimension=0, tiled=True
        ).astype(jnp.float32),
        lax.psum_scatter(
            acc_merge_bias.astype(jnp.bfloat16), "dp", scatter_dimension=0, tiled=True
        ).astype(jnp.float32),
        lax.psum_scatter(
            acc_gain_two.astype(jnp.bfloat16), "dp", scatter_dimension=0, tiled=True
        ).astype(jnp.float32),
        lax.psum_scatter(
            acc_shift_two.astype(jnp.bfloat16), "dp", scatter_dimension=0, tiled=True
        ).astype(jnp.float32),
        lax.psum_scatter(
            acc_reduce_bias.astype(jnp.bfloat16), "dp", scatter_dimension=0, tiled=True
        ).astype(jnp.float32),
    )
    pair_grad, unit_grad, total_sums = lax.psum((acc_pair_bias, acc_unit_bias, square_sums), "dp")
    root_means = jnp.sqrt(total_sums[:3] / (total_sums[3] * width))
    layer_output = jnp.concatenate(output_parts, axis=0)
    hidden_grad = jnp.concatenate(grad_parts, axis=0)
    return (
        layer_output,
        hidden_grad,
        owned[4],
        owned[5],
        owned[0],
        pair_grad,
        owned[1],
        owned[6],
        owned[7],
        owned[8],
        owned[2],
        unit_grad,
        owned[3],
        owned[9],
        root_means,
    )


def solution(mesh):
    return jax.shard_map(
        local,
        mesh=mesh,
        in_specs=(
            P("dp", None),
            P("dp", None),
            P("dp"),
            P("dp"),
            P("dp"),
            P("dp", None, "mp"),
            P(None, "mp"),
            P("mp", "dp"),
            P("dp"),
            P("dp"),
            P("dp"),
            P("dp", "mp"),
            P("mp"),
            P("mp", "dp"),
            P("dp"),
        ),
        out_specs=(
            P("dp", None),
            P("dp", None),
            P("dp"),
            P("dp"),
            P("dp", None, "mp"),
            P(None, "mp"),
            P("mp", "dp"),
            P("dp"),
            P("dp"),
            P("dp"),
            P("dp", "mp"),
            P("mp"),
            P("mp", "dp"),
            P("dp"),
            P(),
        ),
        check_vma=False,
    )
```

profile of v0, /device:TPU:0, one launch (start us, length us, event | category | flops | bytes accessed | tf_op | source)
XLA Modules:
  0.0 1231.0 jit_solution(12049603003931523445)
XLA Ops:
  17.5 10.6 all-gather
  37.4 22.4 %all-gather.11.cloned.1.call-done = bf16[2048,3,512]{0,2,1:T(8,128)(2,1)} async-done(((bf16[256,3,512]{0,2,1:T(8,128)(2,1)}), bf16[2048,3,512]{0,2,1:T(8,128)(2,1)}) %all-gather.11.cloned.1.call-update) | async-done | bytes 6291472 | tf_op jit(solution)/shard_map/all_gather | solution.py:64
  73.6 16.2 %all-gather.13.cloned.1.call-done = bf16[512,2048]{1,0:T(8,128)(2,1)} async-done(((bf16[512,256]{1,0:T(8,128)(2,1)}), bf16[512,2048]{1,0:T(8,128)(2,1)}) %all-gather.13.cloned.1.call-update) | async-done | bytes 2097168 | tf_op jit(solution)/shard_map/all_gather | solution.py:65
  104.3 76.0 %all-reduce.15.cloned.1.call-done = bf16[512,2048]{1,0:T(8,128)(2,1)} async-done(((bf16[512,2048]{1,0:T(8,128)(2,1)}), bf16[512,2048]{1,0:T(8,128)(2,1)}) %all-reduce.15.cloned.1.call-update) | async-done | bytes 2097168 | tf_op jit(solution)/shard_map/psum | solution.py:118
  221.1 66.0 %all-reduce.17.cloned.1.call-done = bf16[512,2048]{1,0:T(8,128)(2,1)} async-done(((bf16[512,2048]{1,0:T(8,128)(2,1)}), bf16[512,2048]{1,0:T(8,128)(2,1)}) %all-reduce.17.cloned.1.call-update) | async-done | bytes 2097168 | tf_op jit(solution)/shard_map/psum | solution.py:118
  293.0 49.2 %all-gather.15.cloned.1.call-done = bf16[2048,2048]{1,0:T(8,128)(2,1)} async-done(((bf16[256,2048]{1,0:T(8,128)(2,1)}), bf16[2048,2048]{1,0:T(8,128)(2,1)}) %all-gather.15.cloned.1.call-update) | async-done | bytes 8388624 | tf_op jit(solution)/shard_map/all_gather | solution.py:71
  353.0 26.4 %multiply_convert_fusion.3 = (bf16[512,2048]{1,0:T(8,128)(2,1)}, f32[512,2048]{1,0:T(8,128)}, bf16[512,2048]{1,0:T(8,128)(2,1)}, f32[512,2048]{1,0:T(8,128)}, f32[512,2048]{1,0:T(8,128)}) fusion(f32[2048]{0:T(1024)S(1)} %convert_element_type.369, f32[512,2048]{1,0:T(8,128)S(1)} %fusion.108, bf16[2048,2048]{1,0:T(8,128)(2,1)S(1)} %copy-done.105, ...), kind=kOutput, calls=%fused_computation.120 | convolution fusion | flops 4442816512 | bytes 33591296 | tf_op jit(solution)/shard_map/dot_general | solution.py:124
  379.4 20.4 %all-gather.17.cloned.1.call-done = bf16[2048,2048]{1,0:T(8,128)(2,1)} async-done(((bf16[2048,256]{1,0:T(8,128)(2,1)}), bf16[2048,2048]{1,0:T(8,128)(2,1)}) %all-gather.17.cloned.1.call-update) | async-done | bytes 8388624 | tf_op jit(solution)/shard_map/all_gather | solution.py:72
  399.8 12.9 %convert_reduce_fusion.6 = (f32[2048]{0:T(1024)}, bf16[512,2048]{1,0:T(8,128)(2,1)S(1)}) fusion(f32[512,2048]{1,0:T(8,128)} %get-tuple-element.85, bf16[2048,2048]{1,0:T(8,128)(2,1)} %all-gather.17.cloned.1.call-done, pred[512]{0:T(512)(128)(4,1)S(1)} %iota_compare_fusion.1, bf16[1024,2048]{1,0:T(8,128)(2,1)} %param.16, f32[512,2048]{1,0:T(8,128)} %copy-done.120, ...), kind=kOutput, calls=%fused_computation.81 | convolution fusion | flops 4315936768 | bytes 20988416 | tf_op jit(solution)/shard_map/dot_general | solution.py:146
  412.7 9.9 convolution_convert_fusion
  422.6 11.5 convert_reduce_fusion.7
  434.1 10.0 convolution_convert_fusion.1
  468.9 281.5 %all-reduce.21.cloned.1.call-done = (bf16[512,2048]{1,0:T(8,128)(2,1)}, bf16[512,2048]{1,0:T(8,128)(2,1)}, bf16[512,2048]{1,0:T(8,128)(2,1)}, bf16[512,2048]{1,0:T(8,128)(2,1)}) async-done(((bf16[512,2048]{1,0:T(8,128)(2,1)}, bf16[512,2048]{1,0:T(8,128)(2,1)}, bf16[512,2048]{1,0:T(8,128)(2,1)}, bf16[512,2048]{1,0:T(8,128)(2,1)}), (bf16[512,2048]{1,0:T(8,128)(2,1)}, bf16[512,2048]{1,0:T(8,128)(2,1)}, ...) | async-done | bytes 8388624 | tf_op jit(solution)/shard_map/psum | solution.py:127
  750.5 14.7 %select_reduce_fusion.5 = (f32[]{:T(128)}, f32[512]{0:T(512)S(1)}, f32[512]{0:T(512)S(1)}, f32[]{:T(128)}, f32[]{:T(128)}, /*index=5*/f32[]{:T(128)}, f32[]{:T(1...) fusion(bf16[512,2048]{1,0:T(8,128)(2,1)} %get-tuple-element.67,, ...), kind=kLoop, calls=%fused_computation.80 | loop fusion | flops 55567360 | bytes 25224216 | tf_op jit(solution)/shard_map/reduce_sum | solution.py:134
  854.1 13.8 %fusion.106 = f32[2048,2048]{1,0:T(8,128)} fusion(bf16[512,2048]{1,0:T(8,128)(2,1)} %copy-done.119, f32[2048]{0:T(1024)S(1)} %bitcast.180, f32[2048]{0:T(1024)S(1)} %bitcast.161, f32[512]{0:T(512)S(1)} %copy-done.74, bf16[512,2048]{1,0:T(8,128)(2,1)} %all-reduce.15.cloned.1.call-done, f32[512]{0:T(512)S(1)} %broadcast_multiply_fusion.3, ...), kind=kOutput, calls=%fused_computation.249 | convolution fusion | flops 4304404480 | bytes 23097344 | tf_op jit(solution)/shard_map/dot_general | solution.py:150
  867.9 15.6 %add_convert_fusion.1 = bf16[2048,2048]{1,0:T(8,128)(2,1)} fusion(f32[2048,2048]{1,0:T(8,128)} %fusion.106, bf16[512,2048]{1,0:T(8,128)(2,1)} %copy-done.121, f32[512]{0:T(512)S(1)} %copy-done.72, f32[2048]{0:T(1024)S(1)} %bitcast.181, f32[2048]{0:T(1024)S(1)} %bitcast.162, bf16[512,2048]{1,0:T(8,128)(2,1)} %all-reduce.17.cloned.1.call-done, ...), kind=kOutput, calls=%fused_computation.1 | convolution fusion | flops 4312793088 | bytes 31485952 | tf_op jit(solution)/shard_map/dot_general | solution.py:150
  885.0 10.0 fusion.71
  895.0 11.0 add_convert_fusion
  931.9 25.5 %all-reduce.6 = (f32[2,512]{1,0:T(2,128)}, f32[2048]{0:T(1024)}, f32[4]{0:T(128)S(1)}) all-reduce(f32[2,512]{1,0:T(2,128)S(1)} %maximum_add_fusion, f32[2048]{0:T(1024)S(1)} %add.360, f32[4]{0:T(128)S(1)} %maximum_add_fusion.1), channel_id=1, replica_groups=mesh['dp'=8,'mp'=4] {'dp'}, use_global_device_ids=true, to_apply=%region_41.42 | all-reduce | flops 3076 | bytes 24608 | tf_op jit(solution)/shard_map/psum | solution.py:240
  965.2 42.5 %all-reduce.19.cloned.1.call-done = (bf16[512,2048]{1,0:T(8,128)(2,1)}, bf16[512,2048]{1,0:T(8,128)(2,1)}) async-done(((bf16[512,2048]{1,0:T(8,128)(2,1)}, bf16[512,2048]{1,0:T(8,128)(2,1)}), (bf16[512,2048]{1,0:T(8,128)(2,1)}, bf16[512,2048]{1,0:T(8,128)(2,1)})) %all-reduce.19.cloned.1.call-update) | async-done | bytes 4194320 | tf_op jit(solution)/shard_map/psum | solution.py:201
  1017.6 24.3 %all-reduce.7 = (bf16[2048]{0:T(1024)(128)(2,1)S(1)}, bf16[2048]{0:T(1024)(128)(2,1)S(1)}, bf16[2048]{0:T(1024)(128)(2,1)S(1)}, bf16[2048]{0:T(1024)(128)(2,1)S(...) all-reduce(bf16[2048]{0:T(1024)(128)(2,1)S(1)} %add_convert_fusion., ...), channel_id=2, replica_groups=mesh['dp'=8,'mp'=4] {'dp'}, use_global_device_ids=true, to_apply=%region_32.33.clone | all-reduce | flops 12288 | bytes 49152
  1062.7 18.8 %reduce-scatter.9.cloned.1.call-done = bf16[256,2048]{1,0:T(8,128)(2,1)} async-done(((bf16[2048,2048]{1,0:T(8,128)(2,1)}), bf16[256,2048]{1,0:T(8,128)(2,1)}) %reduce-scatter.9.cloned.1.call-update) | async-done | bytes 1048592 | tf_op jit(solution)/shard_map/reduce_scatter | solution.py:215
  1084.3 72.0 %reduce-scatter.11.cloned.1.call-done = bf16[2048,256]{1,0:T(8,128)(2,1)} async-done(((bf16[2048,2048]{1,0:T(8,128)(2,1)}), bf16[2048,256]{1,0:T(8,128)(2,1)}) %reduce-scatter.11.cloned.1.call-update) | async-done | bytes 1048592 | tf_op jit(solution)/shard_map/reduce_scatter | solution.py:218
  1159.0 62.2 %reduce-scatter.5.cloned.1.call-done = bf16[256,3,512]{2,0,1:T(8,128)(2,1)} async-done(((bf16[2048,3,512]{2,0,1:T(8,128)(2,1)}), bf16[256,3,512]{2,0,1:T(8,128)(2,1)}) %reduce-scatter.5.cloned.1.call-update) | async-done | bytes 786448 | tf_op jit(solution)/shard_map/reduce_scatter | solution.py:209
  (414 shorter events, 288.6 us)
Async XLA Ops:
  7.2 52.6 %all-gather.11.cloned.1.call-start = ((), (), s32[]{:S(2)}) async-start(), calls=%async_computation.4 | async-start | bytes 7077888 | tf_op jit(solution)/shard_map/all_gather | solution.py:64
  9.6 80.3 %all-gather.13.cloned.1.call-start = ((), (), s32[]{:S(2)}) async-start(), calls=%async_computation.5 | async-start | bytes 2359296 | tf_op jit(solution)/shard_map/all_gather | solution.py:65
  10.3 170.0 %all-reduce.15.cloned.1.call-start = ((), (), s32[]{:S(2)}) async-start(), calls=%async_computation.6 | async-start | bytes 4194304 | tf_op jit(solution)/shard_map/psum | solution.py:118
  17.4 753.8 %copy-start.97 = (pred[512]{0:T(512)(128)(4,1)}, pred[512]{0:T(512)(128)(4,1)S(1)}, u32[]{:S(2)}) copy-start(pred[512]{0:T(512)(128)(4,1)S(1)} %iota_compare_fusion.2) | copy-start | bytes 1540
  28.1 156.6 %copy-start.56 = (f32[8,1,256]{2,1,0:T(1,128)}, f32[8,1,256]{2,1,0:T(1,128)S(1)}, u32[]{:S(2)}) copy-start(f32[8,1,256]{2,1,0:T(1,128)S(1)} %convert_element_type.455) | copy-start | bytes 24580
  37.0 147.7 %copy-start.93 = (f32[8,1,256]{2,1,0:T(1,128)}, f32[8,1,256]{2,1,0:T(1,128)S(1)}, u32[]{:S(2)}) copy-start(f32[8,1,256]{2,1,0:T(1,128)S(1)} %convert_element_type.456) | copy-start | bytes 24580
  37.1 154.4 %copy-start.64 = (f32[8,64]{1,0:T(8,128)}, f32[8,64]{1,0:T(8,128)S(1)}, u32[]{:S(2)}) copy-start(f32[8,64]{1,0:T(8,128)S(1)} %add.314) | copy-start | bytes 6148
  37.2 157.8 %copy-start.58 = (f32[8,64]{1,0:T(8,128)}, f32[8,64]{1,0:T(8,128)S(1)}, u32[]{:S(2)}) copy-start(f32[8,64]{1,0:T(8,128)S(1)} %add.311) | copy-start | bytes 6148
  73.6 111.1 %copy-start.39 = (bf16[8,64,512]{2,1,0:T(8,128)(2,1)}, bf16[8,64,512]{2,1,0:T(8,128)(2,1)S(1)}, u32[]{:S(2)}) copy-start(bf16[8,64,512]{2,1,0:T(8,128)(2,1)S(1)} %convolution_convert_fusion.11) | copy-start | bytes 1572868
  94.0 193.1 %all-reduce.17.cloned.1.call-start = ((), (), s32[]{:S(2)}) async-start(), calls=%async_computation.9 | async-start | bytes 4194304 | tf_op jit(solution)/shard_map/psum | solution.py:118
  104.1 646.3 %copy-start.99 = (pred[512]{0:T(512)(128)(4,1)}, pred[512]{0:T(512)(128)(4,1)S(1)}, u32[]{:S(2)}) copy-start(pred[512]{0:T(512)(128)(4,1)S(1)} %iota_compare_fusion.1) | copy-start | bytes 1540
  104.2 87.1 %copy-start.60 = (f32[512]{0:T(512)}, f32[512]{0:T(512)S(1)}, u32[]{:S(2)}) copy-start(f32[512]{0:T(512)S(1)} %broadcast_multiply_fusion.2) | copy-start | bytes 6148
  199.2 88.0 %copy-start.10 = (bf16[512,2048]{1,0:T(8,128)(2,1)S(1)}, bf16[512,2048]{1,0:T(8,128)(2,1)}, u32[]{:S(2)}) copy-start(bf16[512,2048]{1,0:T(8,128)(2,1)} %all-reduce.15.cloned.1.call-done) | copy-start | bytes 6291460
  201.8 140.4 %all-gather.15.cloned.1.call-start = ((), (), s32[]{:S(2)}) async-start(), calls=%async_computation.7 | async-start | bytes 9437184 | tf_op jit(solution)/shard_map/all_gather | solution.py:71
  202.4 197.4 %all-gather.17.cloned.1.call-start = ((), (), s32[]{:S(2)}) async-start(), calls=%async_computation.8 | async-start | bytes 9437184 | tf_op jit(solution)/shard_map/all_gather | solution.py:72
  203.0 547.5 %all-reduce.21.cloned.1.call-start = ((), (), s32[]{:S(2)}) async-start(), calls=%async_computation.15 | async-start | bytes 16777216 | tf_op jit(solution)/shard_map/psum | solution.py:127
  221.0 129.9 %copy-start.95 = (f32[8,1,256]{2,1,0:T(1,128)}, f32[8,1,256]{2,1,0:T(1,128)S(1)}, u32[]{:S(2)}) copy-start(f32[8,1,256]{2,1,0:T(1,128)S(1)} %convert_element_type.459) | copy-start | bytes 24580
  292.9 498.5 %copy-start.71 = (f32[512]{0:T(512)}, f32[512]{0:T(512)S(1)}, u32[]{:S(2)}) copy-start(f32[512]{0:T(512)S(1)} %fusion.93) | copy-start | bytes 6148
  292.9 478.3 %copy-start.73 = (f32[512]{0:T(512)}, f32[512]{0:T(512)S(1)}, u32[]{:S(2)}) copy-start(f32[512]{0:T(512)S(1)} %fusion.91) | copy-start | bytes 6148
  459.4 504.0 %reduce-scatter.7.cloned.1.call-start = ((), (), s32[]{:S(2)}) async-start(), calls=%async_computation.11 | async-start | bytes 2359296 | tf_op jit(solution)/shard_map/reduce_scatter | solution.py:212
  803.4 204.2 %all-reduce.19.cloned.1.call-start = ((), (), s32[]{:S(2)}) async-start(), calls=%async_computation.14 | async-start | bytes 8388608 | tf_op jit(solution)/shard_map/psum | solution.py:201
  853.4 228.0 %reduce-scatter.9.cloned.1.call-start = ((), (), s32[]{:S(2)}) async-start(), calls=%async_computation.12 | async-start | bytes 9437184 | tf_op jit(solution)/shard_map/reduce_scatter | solution.py:215
  883.5 272.8 %reduce-scatter.11.cloned.1.call-start = ((), (), s32[]{:S(2)}) async-start(), calls=%async_computation.13 | async-start | bytes 9437184 | tf_op jit(solution)/shard_map/reduce_scatter | solution.py:218
  906.1 315.1 %reduce-scatter.5.cloned.1.call-start = ((), (), s32[]{:S(2)}) async-start(), calls=%async_computation.10 | async-start | bytes 7077888 | tf_op jit(solution)/shard_map/reduce_scatter | solution.py:209
  (116 other events, 1016.1 us)
Sparse Core Ops, SparseCore 0:
  10.5 49.2 all-gather.10
  61.7 28.0 all-gather.12
  94.2 86.1 all-reduce.14
  201.9 85.1 all-reduce.16
  288.9 53.2 all-gather.14
  343.9 55.8 all-gather.16
  459.5 290.8 all-reduce.20
  803.5 40.1 reduce-scatter.6
  853.5 154.0 all-reduce.18
  1010.9 70.5 reduce-scatter.8
  1084.9 71.2 reduce-scatter.10
  1159.5 61.6 reduce-scatter.4
where the time goes:
time: 1240 us; the launch traced here: 1230 us
  waiting for transfers between devices  729 us (59%)
  matrix products  242 us (20%)
  other arithmetic  108 us (9%)
  blocking collectives  105 us (8%)
  local copies, waits for them, and re-layouts  26.2 us (2%)
  between operations  18.9 us (2%)
    psum x1, waiting for transfers between devices, local(): lax.psum(feed_part.astype(jnp.bfloat16), 'mp').astype(jnp.float32)  282 us
    psum x2, waiting for transfers between devices, local(): lax.psum(attention_part.astype(jnp.bfloat16), 'mp').astype(jnp.float32)  142 us
    reduce_scatter x1, waiting for transfers between devices, local(): lax.psum_scatter(acc_reduce.astype(jnp.bfloat16), 'dp', scatter_dimension...  72 us
    reduce_scatter x1, waiting for transfers between devices, local(): lax.psum_scatter(acc_triple.astype(jnp.bfloat16), 'dp', scatter_dimension...  62.2 us
    all_gather x1, waiting for transfers between devices, local(): lax.all_gather(expand_weight, 'dp', axis=0, tiled=True)  49.2 us
    psum x1, waiting for transfers between devices, local(): lax.psum(grad_in_part.astype(jnp.bfloat16), 'mp').astype(jnp.float32)  42.5 us
    dot_general x2, matrix products, local(): jnp.dot(norm_mid, expand_full, preferred_element_type=jnp.float32)  35.1 us
    dot_general x2, matrix products, local(): jnp.dot(norm_mid.T, grad_pre, preferred_element_type=jnp.float32)  29.3 us
  transfers between devices with their start and end apart: 12, of which 11 were waited for; matrix products, arithmetic and copies ran while one was open for 18% of the time, Pallas kernels for 0%

commit v1 on v0

--- a/solution.py
+++ b/solution.py
@@ -115,9 +115,9 @@
         )
         mixed_heads = mixed_heads.reshape(slot, head_cols).astype(jnp.bfloat16)
         attention_part = jnp.dot(mixed_heads, merge_full, preferred_element_type=jnp.float32)
-        attention_branch = lax.psum(attention_part.astype(jnp.bfloat16), "mp").astype(
-            jnp.float32
-        ) + merge_shift.astype(jnp.float32)
+        attention_branch = jnp.sum(
+            lax.all_gather(attention_part.astype(jnp.bfloat16), "mp"), axis=0
+        ).astype(jnp.float32) + merge_shift.astype(jnp.float32)
         residual = token_rows + attention_branch
         norm_mid = layer_norm(residual, gain_two, shift_two).astype(jnp.bfloat16)
         token_count = length.astype(jnp.float32)

time: 1240 us -> 1340 us (1.081)
  waiting for transfers between devices: 729 us -> 819 us
    all_gather x0 -> x2, waiting for transfers between devices: none -> 268 us  [local(): lax.all_gather(attention_part.astype(jnp.bfloat16), 'mp')]
    psum x2 -> x0, waiting for transfers between devices: 142 us -> none  [local(): lax.psum(attention_part.astype(jnp.bfloat16), 'mp').astype(jnp.float32)]
    psum x1, waiting for transfers between devices: 42.5 us -> 155 us  [local(): lax.psum(grad_in_part.astype(jnp.bfloat16), 'mp').astype(jnp.float32)]
    reduce_scatter x1, waiting for transfers between devices: 72 us -> 3.43 us  [local(): lax.psum_scatter(acc_reduce.astype(jnp.bfloat16), 'dp', scatter_dimension...]
    reduce_scatter x1, waiting for transfers between devices: 62.2 us -> 8.59 us  [local(): lax.psum_scatter(acc_triple.astype(jnp.bfloat16), 'dp', scatter_dimension...]
    reduce_scatter x1, waiting for transfers between devices: 18.8 us -> 0.01 us  [local(): lax.psum_scatter(acc_expand.astype(jnp.bfloat16), 'dp', scatter_dimension...]
  transfers between devices with their start and end apart: 12 -> 12, of which waited for: 11 -> 10; matrix products, arithmetic and copies ran while one was open for 18% -> 18% of each run, Pallas kernels for 0% -> 0%
where the time goes in v1:
time: 1340 us; the launch traced here: 1330 us
  waiting for transfers between devices  819 us (61%)
  matrix products  247 us (18%)
  other arithmetic  110 us (8%)
  blocking collectives  106 us (8%)
  local copies, waits for them, and re-layouts  31.1 us (2%)
  between operations  19 us (1%)
    psum x1, waiting for transfers between devices, local(): lax.psum(feed_part.astype(jnp.bfloat16), 'mp').astype(jnp.float32)  282 us
    all_gather x2, waiting for transfers between devices, local(): lax.all_gather(attention_part.astype(jnp.bfloat16), 'mp')  268 us
    psum x1, waiting for transfers between devices, local(): lax.psum(grad_in_part.astype(jnp.bfloat16), 'mp').astype(jnp.float32)  155 us
    all_gather x1, waiting for transfers between devices, local(): lax.all_gather(expand_weight, 'dp', axis=0, tiled=True)  40.6 us
    dot_general x2, matrix products, local(): jnp.dot(norm_mid, expand_full, preferred_element_type=jnp.float32)  34.8 us
    dot_general x2, matrix products, local(): jnp.dot(norm_mid.T, grad_pre, preferred_element_type=jnp.float32)  29.7 us
  transfers between devices with their start and end apart: 12, of which 10 were waited for; matrix products, arithmetic and copies ran while one was open for 18% of the time, Pallas kernels for 0%

profile of v1, /device:TPU:0, one launch (start us, length us, event | category | flops | bytes accessed | tf_op | source)
XLA Modules:
  0.0 1333.2 jit_solution(5852620723753710804)
XLA Ops:
  17.5 10.6 all-gather.2
  37.4 22.4 %all-gather.15.cloned.1.call-done = bf16[2048,3,512]{0,2,1:T(8,128)(2,1)} async-done(((bf16[256,3,512]{0,2,1:T(8,128)(2,1)}), bf16[2048,3,512]{0,2,1:T(8,128)(2,1)}) %all-gather.15.cloned.1.call-update) | async-done | bytes 6291472 | tf_op jit(solution)/shard_map/all_gather | solution.py:64
  73.5 16.3 %all-gather.17.cloned.1.call-done = bf16[512,2048]{1,0:T(8,128)(2,1)} async-done(((bf16[512,256]{1,0:T(8,128)(2,1)}), bf16[512,2048]{1,0:T(8,128)(2,1)}) %all-gather.17.cloned.1.call-update) | async-done | bytes 2097168 | tf_op jit(solution)/shard_map/all_gather | solution.py:65
  104.1 139.8 %all-gather.23.cloned.1.call-done = bf16[2048,2048]{1,0:T(8,128)(2,1)} async-done(((bf16[512,2048]{1,0:T(8,128)(2,1)}), bf16[2048,2048]{1,0:T(8,128)(2,1)}) %all-gather.23.cloned.1.call-update) | async-done | bytes 8388624 | tf_op jit(solution)/shard_map/all_gather | solution.py:119
  271.7 9.4 all-gather.5
  290.1 128.4 %all-gather.25.cloned.1.call-done = bf16[2048,2048]{1,0:T(8,128)(2,1)} async-done(((bf16[512,2048]{1,0:T(8,128)(2,1)}), bf16[2048,2048]{1,0:T(8,128)(2,1)}) %all-gather.25.cloned.1.call-update) | async-done | bytes 8388624 | tf_op jit(solution)/shard_map/all_gather | solution.py:119
  432.0 40.6 %all-gather.19.cloned.1.call-done = bf16[2048,2048]{1,0:T(8,128)(2,1)} async-done(((bf16[256,2048]{1,0:T(8,128)(2,1)}), bf16[2048,2048]{1,0:T(8,128)(2,1)}) %all-gather.19.cloned.1.call-update) | async-done | bytes 8388624 | tf_op jit(solution)/shard_map/all_gather | solution.py:71
  483.3 26.1 %multiply_convert_fusion.3 = (bf16[512,2048]{1,0:T(8,128)(2,1)}, f32[512,2048]{1,0:T(8,128)}, bf16[512,2048]{1,0:T(8,128)(2,1)}, f32[512,2048]{1,0:T(8,128)}, f32[512,2048]{1,0:T(8,128)}) fusion(f32[2048]{0:T(1024)S(1)} %convert_element_type.373, f32[512,2048]{1,0:T(8,128)S(1)} %fusion.108, bf16[2048,2048]{1,0:T(8,128)(2,1)S(1)} %copy-done.93, ...), kind=kOutput, calls=%fused_computation.120 | convolution fusion | flops 4442816512 | bytes 33591296 | tf_op jit(solution)/shard_map/dot_general | solution.py:124
  509.4 20.9 %all-gather.21.cloned.1.call-done = bf16[2048,2048]{1,0:T(8,128)(2,1)} async-done(((bf16[2048,256]{1,0:T(8,128)(2,1)}), bf16[2048,2048]{1,0:T(8,128)(2,1)}) %all-gather.21.cloned.1.call-update) | async-done | bytes 8388624 | tf_op jit(solution)/shard_map/all_gather | solution.py:72
  530.3 12.8 convert_reduce_fusion.6
  543.1 9.9 convolution_convert_fusion
  553.0 11.5 convert_reduce_fusion.7
  564.6 10.0 convolution_convert_fusion.1
  574.5 9.5 convolution_convert_fusion.2
  599.3 281.5 %all-reduce.15.cloned.1.call-done = (bf16[512,2048]{1,0:T(8,128)(2,1)}, bf16[512,2048]{1,0:T(8,128)(2,1)}, bf16[512,2048]{1,0:T(8,128)(2,1)}, bf16[512,2048]{1,0:T(8,128)(2,1)}) async-done(((bf16[512,2048]{1,0:T(8,128)(2,1)}, bf16[512,2048]{1,0:T(8,128)(2,1)}, bf16[512,2048]{1,0:T(8,128)(2,1)}, bf16[512,2048]{1,0:T(8,128)(2,1)}), (bf16[512,2048]{1,0:T(8,128)(2,1)}, bf16[512,2048]{1,0:T(8,128)(2,1)}, ...) | async-done | bytes 8388624 | tf_op jit(solution)/shard_map/psum | solution.py:127
  880.9 14.7 %select_reduce_fusion.5 = (f32[]{:T(128)}, f32[512]{0:T(512)S(1)}, f32[512]{0:T(512)S(1)}, f32[]{:T(128)}, f32[]{:T(128)}, /*index=5*/f32[]{:T(128)}, f32[]{:T(1...) fusion(bf16[512,2048]{1,0:T(8,128)(2,1)} %get-tuple-element.67,, ...), kind=kLoop, calls=%fused_computation.80 | loop fusion | flops 55567360 | bytes 25224216 | tf_op jit(solution)/shard_map/reduce_sum | solution.py:134
  911.5 14.0 %fusion.106 = f32[2048,2048]{1,0:T(8,128)} fusion(bf16[512,2048]{1,0:T(8,128)(2,1)} %copy-done.105, f32[2048]{0:T(1024)S(1)} %bitcast.184, f32[2048]{0:T(1024)S(1)} %bitcast.165, f32[512]{0:T(512)S(1)} %fusion.91, bf16[512,2048]{1,0:T(8,128)(2,1)} %copy-done.10, f32[512]{0:T(512)S(1)} %broadcast_multiply_fusion.3, f32[2048]{0:T(1024)S(1)} %bitcast.155, ...), kind=kOutput, calls=%fused_computation.249 | convolution fusion | flops 4304404480 | bytes 23097344 | tf_op jit(solution)/shard_map/dot_general | solution.py:150
  925.5 15.7 %add_convert_fusion.1 = bf16[2048,2048]{1,0:T(8,128)(2,1)} fusion(f32[2048,2048]{1,0:T(8,128)} %fusion.106, bf16[512,2048]{1,0:T(8,128)(2,1)} %copy-done.107, f32[512]{0:T(512)S(1)} %fusion.93, f32[2048]{0:T(1024)S(1)} %bitcast.185, f32[2048]{0:T(1024)S(1)} %bitcast.166, bf16[512,2048]{1,0:T(8,128)(2,1)} %reduce_sum.428, ...), kind=kOutput, calls=%fused_computation.1 | convolution fusion | flops 4312793088 | bytes 31485952 | tf_op jit(solution)/shard_map/dot_general | solution.py:150
  942.8 10.0 fusion.71
  952.8 11.3 add_convert_fusion
  1036.5 10.0 fusion.70
  1062.2 25.3 %all-reduce.6 = (f32[2,512]{1,0:T(2,128)}, f32[2048]{0:T(1024)}, f32[4]{0:T(128)S(1)}) all-reduce(f32[2,512]{1,0:T(2,128)S(1)} %maximum_add_fusion, f32[2048]{0:T(1024)S(1)} %add.356, f32[4]{0:T(128)S(1)} %maximum_add_fusion.1), channel_id=1, replica_groups=mesh['dp'=8,'mp'=4] {'dp'}, use_global_device_ids=true, to_apply=%region_41.42 | all-reduce | flops 3076 | bytes 24608 | tf_op jit(solution)/shard_map/psum | solution.py:240
  1104.1 155.3 %all-reduce.13.cloned.1.call-done = (bf16[512,2048]{1,0:T(8,128)(2,1)}, bf16[512,2048]{1,0:T(8,128)(2,1)}) async-done(((bf16[512,2048]{1,0:T(8,128)(2,1)}, bf16[512,2048]{1,0:T(8,128)(2,1)}), (bf16[512,2048]{1,0:T(8,128)(2,1)}, bf16[512,2048]{1,0:T(8,128)(2,1)})) %all-reduce.13.cloned.1.call-update) | async-done | bytes 4194320 | tf_op jit(solution)/shard_map/psum | solution.py:201
  1269.5 24.9 %all-reduce.7 = (bf16[2048]{0:T(1024)(128)(2,1)S(1)}, bf16[2048]{0:T(1024)(128)(2,1)S(1)}, bf16[2048]{0:T(1024)(128)(2,1)S(1)}, bf16[2048]{0:T(1024)(128)(2,1)S(...) all-reduce(bf16[2048]{0:T(1024)(128)(2,1)S(1)} %add_convert_fusion., ...), channel_id=4, replica_groups=mesh['dp'=8,'mp'=4] {'dp'}, use_global_device_ids=true, to_apply=%region_32.33.clone | all-reduce | flops 12288 | bytes 49152
  (388 shorter events, 283.5 us)
Async XLA Ops:
  7.2 52.6 %all-gather.15.cloned.1.call-start = ((), (), s32[]{:S(2)}) async-start(), calls=%async_computation.4 | async-start | bytes 7077888 | tf_op jit(solution)/shard_map/all_gather | solution.py:64
  9.6 80.3 %all-gather.17.cloned.1.call-start = ((), (), s32[]{:S(2)}) async-start(), calls=%async_computation.5 | async-start | bytes 2359296 | tf_op jit(solution)/shard_map/all_gather | solution.py:65
  10.3 233.5 %all-gather.23.cloned.1.call-start = ((), (), s32[]{:S(2)}) async-start(), calls=%async_computation.12 | async-start | bytes 10485760 | tf_op jit(solution)/shard_map/all_gather | solution.py:119
  12.3 54.0 %copy-start.64 = (f32[512]{0:T(512)}, f32[512]{0:T(512)S(1)}, u32[]{:S(2)}) copy-start(f32[512]{0:T(512)S(1)} %broadcast_multiply_fusion.4) | copy-start | bytes 6148
  16.1 50.3 %copy-start.76 = (f32[512]{0:T(512)}, f32[512]{0:T(512)S(1)}, u32[]{:S(2)}) copy-start(f32[512]{0:T(512)S(1)} %fusion.90) | copy-start | bytes 6148
  17.4 49.0 %copy-start.88 = (pred[512]{0:T(512)(128)(4,1)}, pred[512]{0:T(512)(128)(4,1)S(1)}, u32[]{:S(2)}) copy-start(pred[512]{0:T(512)(128)(4,1)S(1)} %iota_compare_fusion.2) | copy-start | bytes 1540
  28.1 225.8 %copy-start.58 = (f32[8,1,256]{2,1,0:T(1,128)}, f32[8,1,256]{2,1,0:T(1,128)S(1)}, u32[]{:S(2)}) copy-start(f32[8,1,256]{2,1,0:T(1,128)S(1)} %convert_element_type.459) | copy-start | bytes 24580
  37.0 216.8 %copy-start.86 = (f32[8,1,256]{2,1,0:T(1,128)}, f32[8,1,256]{2,1,0:T(1,128)S(1)}, u32[]{:S(2)}) copy-start(f32[8,1,256]{2,1,0:T(1,128)S(1)} %convert_element_type.460) | copy-start | bytes 24580
  37.1 223.0 %copy-start.66 = (f32[8,64]{1,0:T(8,128)}, f32[8,64]{1,0:T(8,128)S(1)}, u32[]{:S(2)}) copy-start(f32[8,64]{1,0:T(8,128)S(1)} %add.310) | copy-start | bytes 6148
  37.2 226.4 %copy-start.60 = (f32[8,64]{1,0:T(8,128)}, f32[8,64]{1,0:T(8,128)S(1)}, u32[]{:S(2)}) copy-start(f32[8,64]{1,0:T(8,128)S(1)} %add.307) | copy-start | bytes 6148
  73.5 170.3 %copy-start.48 = (bf16[8,64,512]{2,1,0:T(8,128)(2,1)}, bf16[8,64,512]{2,1,0:T(8,128)(2,1)S(1)}, u32[]{:S(2)}) copy-start(bf16[8,64,512]{2,1,0:T(8,128)(2,1)S(1)} %convolution_convert_fusion.11) | copy-start | bytes 1572868
  94.0 324.4 %all-gather.25.cloned.1.call-start = ((), (), s32[]{:S(2)}) async-start(), calls=%async_computation.13 | async-start | bytes 10485760 | tf_op jit(solution)/shard_map/all_gather | solution.py:119
  103.9 150.0 %copy-start.62 = (f32[512]{0:T(512)}, f32[512]{0:T(512)S(1)}, u32[]{:S(2)}) copy-start(f32[512]{0:T(512)S(1)} %broadcast_multiply_fusion.2) | copy-start | bytes 6148
  249.5 651.5 %copy-start.10 = (bf16[512,2048]{1,0:T(8,128)(2,1)}, bf16[512,2048]{1,0:T(8,128)(2,1)S(1)}, u32[]{:S(2)}) copy-start(bf16[512,2048]{1,0:T(8,128)(2,1)S(1)} %reduce_sum.419) | copy-start | bytes 6291460
  270.5 202.2 %all-gather.19.cloned.1.call-start = ((), (), s32[]{:S(2)}) async-start(), calls=%async_computation.6 | async-start | bytes 9437184 | tf_op jit(solution)/shard_map/all_gather | solution.py:71
  271.1 259.2 %all-gather.21.cloned.1.call-start = ((), (), s32[]{:S(2)}) async-start(), calls=%async_computation.7 | async-start | bytes 9437184 | tf_op jit(solution)/shard_map/all_gather | solution.py:72
  271.7 609.2 %all-reduce.15.cloned.1.call-start = ((), (), s32[]{:S(2)}) async-start(), calls=%async_computation.15 | async-start | bytes 16777216 | tf_op jit(solution)/shard_map/psum | solution.py:127
  589.8 503.6 %reduce-scatter.7.cloned.1.call-start = ((), (), s32[]{:S(2)}) async-start(), calls=%async_computation.9 | async-start | bytes 2359296 | tf_op jit(solution)/shard_map/reduce_scatter | solution.py:212
  911.0 184.2 %reduce-scatter.9.cloned.1.call-start = ((), (), s32[]{:S(2)}) async-start(), calls=%async_computation.10 | async-start | bytes 9437184 | tf_op jit(solution)/shard_map/reduce_scatter | solution.py:215
  941.2 160.2 %reduce-scatter.11.cloned.1.call-start = ((), (), s32[]{:S(2)}) async-start(), calls=%async_computation.11 | async-start | bytes 9437184 | tf_op jit(solution)/shard_map/reduce_scatter | solution.py:218
  964.1 295.4 %all-reduce.13.cloned.1.call-start = ((), (), s32[]{:S(2)}) async-start(), calls=%async_computation.14 | async-start | bytes 8388608 | tf_op jit(solution)/shard_map/psum | solution.py:201
  1035.8 287.6 %reduce-scatter.5.cloned.1.call-start = ((), (), s32[]{:S(2)}) async-start(), calls=%async_computation.8 | async-start | bytes 7077888 | tf_op jit(solution)/shard_map/reduce_scatter | solution.py:209
  1055.2 34.1 %copy-start.34 = (bf16[512,2048]{1,0:T(8,128)(2,1)S(1)}, bf16[512,2048]{1,0:T(8,128)(2,1)}, u32[]{:S(2)}) copy-start(bf16[512,2048]{1,0:T(8,128)(2,1)} %get-tuple-element.78) | copy-start | bytes 6291460
  1265.4 32.8 %copy-start.83 = (f32[512]{0:T(512)S(1)}, f32[512]{0:T(512)}, u32[]{:S(2)}) copy-start(f32[512]{0:T(512)} %copy-done.82) | copy-start | bytes 6148
  (102 other events, 696.3 us)
Sparse Core Ops, SparseCore 0:
  10.5 49.2 all-gather.14
  61.7 28.0 all-gather.16
  94.2 149.5 all-gather.22
  270.6 147.7 all-gather.24
  420.2 52.4 all-gather.18
  474.4 55.8 all-gather.20
  589.9 290.8 all-reduce.14
  911.1 40.1 reduce-scatter.6
  954.8 71.5 reduce-scatter.8
  1029.6 71.7 reduce-scatter.10
  1104.4 155.0 all-reduce.12
  1262.7 60.6 reduce-scatter.4
